TPU v7x, 32 devices: a whole 2x2x4 slice. The times are simulated.
32 devices in a mesh: tm: 4 (over y, x), space: 8 (over z, core).
Axes of the slice: x: 2, y: 2, z: 4, core: 2. Of those that a mesh axis runs over, the one named last changes fastest.
Arguments:
- initial_state: float32 [16, 256, 256], P('space'), may hold values from -6 to 6
- capacity: float32 [16, 256, 256], P('space'), may hold values from 0.5 to 2
- source: float32 [16, 256, 256], P('space'), may hold values from -6 to 6
- control: float32 [4, 16], P('tm'), may hold values from -2 to 2
- segment_index: int32 [16, 256], P('space'), may hold values from 0 to 15
Outputs:
- slice_ends: float32 [4, 16, 256, 256], P('tm', 'space')
All inputs are finite; a program needn't handle non-finite values.
Results may differ from a plain program's by a relative error of at most 0.0001.
Values sent between devices are 32-bit elements; how exact they have to be, the bound alone decides.
A program may use at most 64 MiB of HBM per device.

v0:
```python
import functools

import jax
import jax.numpy as jnp
from jax import lax
from jax.experimental import pallas as pl
from jax.experimental.pallas import tpu as pltpu
from jax.sharding import PartitionSpec as P

SWEEPS = 6
CORRECTIONS = 2
step_fine = 1.0
step_coarse = 0.08


def make_plan(slices):
    last = CORRECTIONS
    solves = [
        (k, n)
        for k in range(last)
        for n in range(k, slices)
        if k == last - 1 or n + 1 < slices or n == k
    ]
    slots, sent = {}, set()
    for k, n in solves:
        for j in range(SWEEPS):
            slots[(k, n, j)] = len(slots)
            sent.add((k, n, j))

    def state(k, n):
        k = min(k, n)
        key = (k, n, 0)
        if key not in slots:
            slots[key] = len(slots)
        return key

    ends = [state(last, n + 1) for n in range(slices)]
    rounds = {}
    top_coarse = max(n for k, n in solves if k == 0)
    for n in range(top_coarse):
        rounds.setdefault(n + 1, []).append(("coarse", n, state(0, n), state(0, n + 1)))
    for k, n in sorted(solves, key=lambda item: (-item[0], item[1])):
        begin = SWEEPS * k + n - k
        for j in range(1, SWEEPS + 1):
            target = (k, n, j) if j < SWEEPS else state(k + 1, n + 1)
            pair = None
            if j == SWEEPS and k < n:
                pair = (state(k + 1, n), state(k, n))
                sent.add(pair[0])
                sent.add(pair[1])
            rounds.setdefault(begin + j, []).append(("sweep", n, (k, n, j - 1), target, j, pair))
    return slots, sent, [rounds[r] for r in sorted(rounds)], ends


def kernel(plan, size, state_hbm, cap_hbm, src_hbm, ctrl_ref, seg_ref, out_hbm,
           field, forcing, base, inv, scale, source, ctrl_all,
           send_sem, recv_sem, in_sem, ctrl_send, ctrl_recv, out_send, out_recv, own_sem):
    slots, sent, rounds, ends = plan
    planes, window, own_rows, reach, rows, cols, slices, count = size
    t = lax.axis_index("tm")
    s = lax.axis_index("space")
    low_there, high_there = s > 0, s < count - 1
    first_row = pl.multiple_of(jnp.clip(t * own_rows - reach, 0, rows - window), 8)
    own_at = pl.multiple_of(t * own_rows - first_row, 8)
    inner = pl.ds(1, planes)
    first = slots[(0, 0, 0)]

    loads = []
    for index, (ref, target) in enumerate(
        ((state_hbm, field.at[first, inner]), (cap_hbm, inv), (src_hbm, source))
    ):
        loads.append(pltpu.make_async_copy(ref.at[:, pl.ds(first_row, window), :], target, in_sem.at[index]))
        loads[-1].start()

    @pl.when(jnp.logical_not(low_there))
    def _():
        for key in sorted(sent):
            field[slots[key], 0] = jnp.zeros((window, cols), jnp.float32)

    @pl.when(jnp.logical_not(high_there))
    def _():
        for key in sorted(sent):
            field[slots[key], planes + 1] = jnp.zeros((window, cols), jnp.float32)

    barrier = pltpu.get_barrier_semaphore()

    @pl.when(low_there)
    def _():
        pl.semaphore_signal(barrier, inc=1, device_id={"space": s - 1})

    @pl.when(high_there)
    def _():
        pl.semaphore_signal(barrier, inc=1, device_id={"space": s + 1})

    for hop in range(1, slices):
        pl.semaphore_signal(barrier, inc=1, device_id={"tm": lax.rem(t + hop, slices)})
    pl.semaphore_wait(barrier, slices - 1 + jnp.minimum(s, 1) + jnp.minimum(count - 1 - s, 1))

    def halo(key, side):
        slot = slots[key]
        if side == 0:
            source_plane, target_plane, other = 1, planes + 1, s - 1
        else:
            source_plane, target_plane, other = planes, 0, s + 1
        k, n, j = key
        left = CORRECTIONS * (SWEEPS - 1) + slices - (k * (SWEEPS - 1) + n + j)
        near = min(-(-left // 8) * 8, reach)
        height = min(window, own_rows + 2 * near)
        at = jnp.clip(t * own_rows - near, 0, rows - height) - first_row
        needed = pl.ds(pl.multiple_of(at, 8), height)
        return pltpu.make_async_remote_copy(
            src_ref=field.at[slot, source_plane, needed],
            dst_ref=field.at[slot, target_plane, needed],
            send_sem=send_sem.at[slot, side],
            recv_sem=recv_sem.at[slot, side],
            device_id={"space": other},
        )

    odd = lax.rem(s, 2)

    def send(key, parts=(0, 1)):
        if key in sent:
            for part in parts:
                for side, there in ((0, low_there), (1, high_there)):

                    @pl.when(jnp.logical_and(there, odd == (side + part) % 2))
                    def _():
                        halo(key, side).start()

    arrived = set()

    def arrive(key):
        if key in arrived:
            return
        arrived.add(key)
        for side, there in ((0, high_there), (1, low_there)):

            @pl.when(there)
            def _():
                halo(key, side).wait_recv()

    loads[0].wait()
    send((0, 0, 0))

    ctrl_copies = []
    for hop in range(1, slices):
        ctrl_copies.append(pltpu.make_async_remote_copy(
            src_ref=ctrl_ref,
            dst_ref=ctrl_all.at[hop],
            send_sem=ctrl_send.at[hop],
            recv_sem=ctrl_recv.at[hop],
            device_id={"tm": lax.rem(t + hop, slices)},
        ))
        ctrl_copies[-1].start()
    own_ctrl = pltpu.make_async_copy(ctrl_ref, ctrl_all.at[0], own_sem.at[0])
    own_ctrl.start()

    loads[1].wait()
    capacity = inv[...]
    scale[...] = step_coarse / capacity
    reciprocal = 1.0 / (capacity + 6.0 * step_fine)
    inv[...] = reciprocal
    loads[2].wait()
    own_ctrl.wait()
    for copy in ctrl_copies:
        copy.wait_recv()

    segment = seg_ref[...]
    segments = ctrl_ref.shape[1]
    row_id = lax.broadcasted_iota(jnp.int32, (planes, window, cols), 1) + first_row
    for n in range(slices):
        row = jnp.zeros((1, segments), jnp.float32)
        for hop in range(slices):
            row = jnp.where(lax.rem(t - n + slices, slices) == hop, ctrl_all[hop], row)
        values = jnp.zeros((planes, cols), jnp.float32)
        for k in range(segments):
            values = jnp.where(segment == k, row[:, k:k + 1], values)
        forcing[n] = source[...] + jnp.where(row_id == 0, values[:, None, :], 0.0)

    step = window // 2 if window % 16 == 0 else window
    lane = lax.broadcasted_iota(jnp.int32, (step, cols), 1)
    line = lax.broadcasted_iota(jnp.int32, (step, cols), 0)
    pieces = []
    for i in range(planes):
        p = jnp.where(odd == 1, planes - 1 - i, i)
        pieces += [(i, p, r) for r in range(0, window, step)]

    def neighbours(read, p, r):
        core = read(p + 1, r)
        if r > 0:
            above = read(p + 1, r - 1)
        else:
            above = jnp.where(line == 0, 0.0, pltpu.roll(core, 1, 0))
        if r + step < window:
            below = read(p + 1, r + 1)
        else:
            below = jnp.where(line == step - 1, 0.0, pltpu.roll(core, step - 1, 0))
        left = jnp.where(lane == 0, 0.0, pltpu.roll(core, 1, 1))
        right = jnp.where(lane == cols - 1, 0.0, pltpu.roll(core, cols - 1, 1))
        return core, read(p, r) + read(p + 2, r) + above + below + left + right

    def reader(key):
        return lambda p, r: field[slots[key], p, pl.ds(r, step)]

    def difference(new, old):
        return lambda p, r: field[slots[new], p, pl.ds(r, step)] - field[slots[old], p, pl.ds(r, step)]

    def piece(ref, p, r):
        return ref[p, pl.ds(r, step)]

    def result(n, end):
        def remote(target, source_slice):
            return pltpu.make_async_remote_copy(
                src_ref=field.at[slots[end], inner, pl.ds(own_at, own_rows)],
                dst_ref=out_hbm.at[0, :, pl.ds(pl.multiple_of(source_slice * own_rows, 8), own_rows)],
                send_sem=out_send.at[target],
                recv_sem=out_recv.at[source_slice],
                device_id={"tm": target},
            )
        return remote

    def own_copy(n):
        return pltpu.make_async_copy(
            field.at[slots[ends[n]], inner, pl.ds(own_at, own_rows)],
            out_hbm.at[0, :, pl.ds(n * own_rows, own_rows)],
            own_sem.at[1],
        )

    def emit(key):
        for n, end in enumerate(ends):
            if end == key:

                @pl.when(t != n)
                def _():
                    result(n, end)(n, t).start()

                @pl.when(t == n)
                def _():
                    own_copy(n).start()

    for tasks in rounds:
        for task in tasks:
            if task[0] == "coarse":
                _, n, source_key, target = task
                arrive(source_key)
                for i, p, r in pieces:
                    core, around = neighbours(reader(source_key), p, r)
                    field[slots[target], p + 1, pl.ds(r, step)] = core + piece(scale, p, r) * (
                        around - 6.0 * core + piece(forcing.at[n], p, r)
                    )
                    if i == 0 and r + step == window:
                        send(target, (0,))
            else:
                _, n, source_key, target, j, pair = task
                held = source_key[0] % 2 * slices + n
                arrive(source_key)
                if pair is not None:
                    arrive(pair[0])
                    arrive(pair[1])
                for i, p, r in pieces:
                    core, around = neighbours(reader(source_key), p, r)
                    gain = piece(inv, p, r)
                    if j == 1:
                        constant = core - gain * (6.0 * step_fine * core - step_fine * piece(forcing.at[n], p, r))
                        base[held, p, pl.ds(r, step)] = constant
                    else:
                        constant = piece(base.at[held], p, r)
                    value = constant + step_fine * gain * around
                    if pair is not None:
                        change, spread = neighbours(difference(*pair), p, r)
                        value = value + change + piece(scale, p, r) * (spread - 6.0 * change)
                    field[slots[target], p + 1, pl.ds(r, step)] = value
                    if i == 0 and r + step == window:
                        send(target, (0,))
            send(target, (1,))
            emit(target)

    for key in sorted(sent):
        arrive(key)
        for side, there in ((0, low_there), (1, high_there)):

            @pl.when(there)
            def _():
                halo(key, side).wait_send()

    for copy in ctrl_copies:
        copy.wait_send()
    for n in range(slices):

        @pl.when(t != n)
        def _():
            result(n, ends[n])(n, t).wait_send()
            result(n, ends[n])(t, n).wait_recv()

        @pl.when(t == n)
        def _():
            own_copy(n).wait()


def solution(mesh):
    slices, count = mesh.shape["tm"], mesh.shape["space"]
    plan = make_plan(slices)

    def on_device(initial_state, capacity, source, control, segment_index):
        planes, rows, cols = initial_state.shape
        own_rows = rows // slices
        reach = -(-(CORRECTIONS * SWEEPS + slices - CORRECTIONS) // 8) * 8
        window = min(rows, own_rows + 2 * reach)
        fields = len(plan[0])
        size = (planes, window, own_rows, reach, rows, cols, slices, count)
        block = (planes, window, cols)
        dma = pltpu.SemaphoreType.DMA
        return pl.pallas_call(
            functools.partial(kernel, plan, size),
            out_shape=jax.ShapeDtypeStruct((1, planes, rows, cols), jnp.float32),
            in_specs=[pl.BlockSpec(memory_space=pl.ANY)] * 3 + [pl.BlockSpec(memory_space=pltpu.VMEM)] * 2,
            out_specs=pl.BlockSpec(memory_space=pl.ANY),
            scratch_shapes=[
                pltpu.VMEM((fields, planes + 2, window, cols), jnp.float32),
                pltpu.VMEM((slices,) + block, jnp.float32),
                pltpu.VMEM((2 * slices,) + block, jnp.float32),
                pltpu.VMEM(block, jnp.float32),
                pltpu.VMEM(block, jnp.float32),
                pltpu.VMEM(block, jnp.float32),
                pltpu.VMEM((slices,) + control.shape, jnp.float32),
                dma((fields, 2)),
                dma((fields, 2)),
                dma((3,)),
                dma((slices,)),
                dma((slices,)),
                dma((slices,)),
                dma((slices,)),
                dma((2,)),
            ],
            compiler_params=pltpu.CompilerParams(
                collective_id=0, has_side_effects=True, vmem_limit_bytes=67043328 - 1048576
            ),
        )(initial_state, capacity, source, control, segment_index)

    return jax.shard_map(
        on_device,
        mesh=mesh,
        in_specs=(
            P("space", None, None),
            P("space", None, None),
            P("space", None, None),
            P("tm", None),
            P("space", None),
        ),
        out_specs=P("tm", "space", None, None),
        check_vma=False,
    )
```

profile of v0, /device:TPU:23, one launch (start us, length us, event | category | flops | bytes accessed | tf_op | source)
XLA Modules:
  0.0 63.3 jit_solution(13040109496753370785)
XLA Ops:
  0.0 61.5 %shard_map.55 = f32[1,2,256,256]{3,2,1,0:T(8,128)} custom-call(f32[2,256,256]{2,1,0:T(8,128)} %state_hbm.1, f32[2,256,256]{2,1,0:T(8,128)} %cap_hbm.1, f32[2,256,256]{2,1,0:T(8,128)} %src_hbm.1, f32[1,16]{1,0:T(1,128)} %ctrl_ref.1, s32[2,256]{1,0:T(2,128)} %seg_ref.1), custom_call_target="tpu_custom_call" | custom-call | tf_op jit(solution)/shard_map/pallas_call | solution.py:313
  61.5 1.9 %copy.7 = f32[1,2,256,256]{3,2,1,0:T(8,128)} copy(f32[1,2,256,256]{3,2,1,0:T(8,128)} %shard_map.55) | data formatting | bytes 1048576
where the time goes:
time: 63.5 us; the launch traced here: 63.3 us
  Pallas kernels  61.5 us (97%)
  local copies, waits for them, and re-layouts  1.87 us (3%)
    pallas_call x1, Pallas kernels, on_device(): pl.pallas_call(functools.partial(kernel, plan, size), out_shape=jax.Shape...  61.5 us
    unnamed x1, local copies, waits for them, and re-layouts  1.87 us

commit v1 on v0

--- a/solution.py
+++ b/solution.py
@@ -297,12 +297,413 @@
             own_copy(n).wait()
 
 
+def wide_kernel(size, state_hbm, cap_hbm, src_hbm, ctrl_ref, seg_ref, out_hbm,
+                stage, given, inv, scale, bounds, coarse, sweep, base, near, change, state, end,
+                seg_all, ctrl_all, load_sem, own_sem, in_send, in_recv, seg_send, seg_recv,
+                ctrl_send, ctrl_recv, side_send, side_recv, mid_send, mid_recv,
+                out_send, out_recv, last_sem):
+    planes, rows, cols, slices, count, own = size
+    total = planes * count
+    devices = slices * count
+    window = 3 * own
+    mine = pl.ds(own, own)
+    whole = pl.ds(1, total)
+    t = lax.axis_index("tm")
+    s = lax.axis_index("space")
+
+    def swap(x):
+        return x + x % 4 // 2 * (1 - 2 * (x % 2))
+
+    def turn(x, level):
+        return x + level % 2 * (slices - 1 - 2 * x)
+
+    def index(t, s):
+        chip = s // 2 * slices + turn(swap(t), s // 2)
+        return 2 * chip + (s + chip) % 2
+
+    def place(i):
+        chip = i // 2
+        level = chip // slices
+        return swap(turn(chip % slices, level)), 2 * level + (i + chip) % 2
+
+    here = index(t, s)
+    has_low, has_high = here > 0, here < devices - 1
+
+    def block(i):
+        return pl.ds(pl.multiple_of(i * own, own), own)
+
+    inputs = (state_hbm, cap_hbm, src_hbm)
+    order = (1, 0, 2)
+    loads = [pltpu.make_async_copy(inputs[a], stage.at[a], load_sem.at[a]) for a in range(3)]
+    owns = [
+        pltpu.make_async_copy(
+            inputs[a].at[:, block(here)], given.at[a, pl.ds(1 + planes * s, planes), mine], own_sem.at[a]
+        )
+        for a in range(3)
+    ]
+    for a in order:
+        loads[a].start()
+    for a in order:
+        owns[a].start()
+    own_seg = pltpu.make_async_copy(seg_ref, seg_all.at[s], own_sem.at[3])
+    own_ctrl = pltpu.make_async_copy(ctrl_ref, ctrl_all.at[0], own_sem.at[4])
+
+    seg_all[...] = jnp.zeros(seg_all.shape, jnp.int32)
+    barrier = pltpu.get_barrier_semaphore()
+    for hop in range(1, count):
+        pl.semaphore_signal(barrier, inc=1, device_id={"space": lax.rem(s + hop, count)})
+    for hop in range(1, slices):
+        pl.semaphore_signal(barrier, inc=1, device_id={"tm": lax.rem(t + hop, slices)})
+
+    flat = jnp.zeros((window, cols), jnp.float32)
+    for plane in (0, total + 1):
+        given[0, plane] = flat
+        for ref in (coarse, sweep, near, change, state, end):
+            for k in range(ref.shape[0]):
+                ref[k, plane] = flat
+    for missing, at in ((has_low, 0), (has_high, 2 * own)):
+
+        @pl.when(jnp.logical_not(missing))
+        def _():
+            side = jnp.zeros((total, own, cols), jnp.float32)
+            given[0, whole, pl.ds(at, own)] = side
+            given[1, whole, pl.ds(at, own)] = side + 1.0
+            given[2, whole, pl.ds(at, own)] = side
+            for k in range(state.shape[0]):
+                state[k, whole, pl.ds(at, own)] = side
+
+    pl.semaphore_wait(barrier, slices + count - 2)
+
+    def spread(a, target, source):
+        return pltpu.make_async_remote_copy(
+            src_ref=stage.at[a, :, block(index(t, target))],
+            dst_ref=given.at[a, pl.ds(1 + planes * source, planes), mine],
+            send_sem=in_send.at[a, target],
+            recv_sem=in_recv.at[a, source],
+            device_id={"space": target},
+        )
+
+    def spread_seg(target, source):
+        return pltpu.make_async_remote_copy(
+            src_ref=seg_ref,
+            dst_ref=seg_all.at[source],
+            send_sem=seg_send.at[target],
+            recv_sem=seg_recv.at[source],
+            device_id={"space": target},
+        )
+
+    def side(make, send_sem, recv_sem, upward):
+        other_t, other_s = place(here + 1 if upward else here - 1)
+        return pltpu.make_async_remote_copy(
+            src_ref=make(own),
+            dst_ref=make(0 if upward else 2 * own),
+            send_sem=send_sem.at[int(upward)],
+            recv_sem=recv_sem.at[int(upward)],
+            device_id={"tm": other_t, "space": other_s},
+        )
+
+    def side_start(*args):
+        for upward, there in ((False, has_low), (True, has_high)):
+
+            @pl.when(there)
+            def _():
+                side(*args, upward).start()
+
+    def side_recv_wait(*args):
+        for upward, there in ((True, has_low), (False, has_high)):
+
+            @pl.when(there)
+            def _():
+                side(*args, upward).wait_recv()
+
+    def side_send_wait(*args):
+        for upward, there in ((False, has_low), (True, has_high)):
+
+            @pl.when(there)
+            def _():
+                side(*args, upward).wait_send()
+
+    def given_side(a):
+        return lambda at: given.at[a, whole, pl.ds(at, own)], side_send.at[a], side_recv.at[a]
+
+    def state_side(n):
+        return lambda at: state.at[n - 1, whole, pl.ds(at, own)], mid_send.at[n - 1], mid_recv.at[n - 1]
+
+    for a in order:
+        loads[a].wait()
+        for hop in range(1, count):
+            target = lax.rem(s + hop, count)
+            spread(a, target, s).start()
+        if a == order[0]:
+            own_seg.start()
+            own_ctrl.start()
+            ctrl_copies = []
+            for hop in range(1, slices):
+                ctrl_copies.append(pltpu.make_async_remote_copy(
+                    src_ref=ctrl_ref,
+                    dst_ref=ctrl_all.at[hop],
+                    send_sem=ctrl_send.at[hop],
+                    recv_sem=ctrl_recv.at[hop],
+                    device_id={"tm": lax.rem(t + hop, slices)},
+                ))
+                ctrl_copies[-1].start()
+            for target in (0, 1):
+
+                @pl.when(jnp.logical_and(t == 0, s != target))
+                def _():
+                    spread_seg(target, s).start()
+
+    row_id = lax.broadcasted_iota(jnp.int32, (window, cols), 0) + (here - 1) * own
+    inside = jnp.logical_and(row_id >= 0, row_id < rows)
+    step = planes
+    spans = [pl.ds(p, step) for p in range(0, total, step)]
+
+    def collect(a):
+        owns[a].wait()
+        for hop in range(1, count):
+            source = lax.rem(s + count - hop, count)
+            spread(a, s, source).wait_recv()
+        side_start(*given_side(a))
+
+    collect(1)
+    collect(0)
+    side_recv_wait(*given_side(1))
+    for p in range(0, total, step):
+        capacity = given[1, pl.ds(p + 1, step)]
+        scale[pl.ds(p, step)] = jnp.where(inside, step_coarse / capacity, 0.0)
+        inv[pl.ds(p, step)] = jnp.where(inside, 1.0 / (capacity + 6.0 * step_fine), 0.0)
+
+    own_seg.wait()
+    own_ctrl.wait()
+    for copy in ctrl_copies:
+        copy.wait_recv()
+    for target in (0, 1):
+
+        @pl.when(jnp.logical_and(t == 0, s == target))
+        def _():
+            for hop in range(1, count):
+                source = (target + hop) % count
+                spread_seg(target, source).wait_recv()
+
+    segments = ctrl_ref.shape[1]
+    for n in range(slices):
+        row = jnp.zeros((1, segments), jnp.float32)
+        for hop in range(slices):
+            row = jnp.where(lax.rem(t - n + slices, slices) == hop, ctrl_all[hop], row)
+        for source in range(count):
+            segment = seg_all[source]
+            values = jnp.zeros((planes, cols), jnp.float32)
+            for k in range(segments):
+                values = jnp.where(segment == k, row[:, k:k + 1], values)
+            bounds[n, pl.ds(source * planes, planes)] = values
+
+    collect(2)
+    side_recv_wait(*given_side(0))
+    side_recv_wait(*given_side(2))
+
+    half = cols // 2
+    lane = lax.broadcasted_iota(jnp.int32, (step, window, half), 2)
+    first_row = row_id == 0
+
+    def around(ref, p):
+        core = ref[pl.ds(p + 1, step)]
+        result = ref[pl.ds(p, step)] + ref[pl.ds(p + 2, step)]
+        result = result + (pltpu.roll(core, 1, 1) + pltpu.roll(core, window - 1, 1))
+        left, right = core[:, :, :half], core[:, :, half:]
+        left_up, right_up = pltpu.roll(left, 1, 2), pltpu.roll(right, 1, 2)
+        left_down, right_down = pltpu.roll(left, half - 1, 2), pltpu.roll(right, half - 1, 2)
+        low = jnp.where(lane == 0, 0.0, left_up) + jnp.where(lane == half - 1, right_down, left_down)
+        high = jnp.where(lane == 0, left_up, right_up) + jnp.where(lane == half - 1, 0.0, right_down)
+        return core, result + jnp.concatenate([low, high], axis=2)
+
+    def forcing(n, p):
+        edge = bounds[n, pl.ds(p, step)][:, None, :]
+        return given[2, pl.ds(p + 1, step)] + jnp.where(first_row[None], edge, 0.0)
+
+    def begin(start, n, target, hold, ahead=None):
+        for p in range(0, total, step):
+            core, spread_sum = around(start, p)
+            gain = inv[pl.ds(p, step)]
+            drive = forcing(n, p) - 6.0 * step_fine * core
+            constant = core + gain * drive
+            hold[pl.ds(p, step)] = constant
+            target[pl.ds(p + 1, step)] = constant + gain * spread_sum
+            if ahead is not None:
+                ahead[pl.ds(p + 1, step)] = core + scale[pl.ds(p, step)] * (drive + spread_sum)
+
+    def go_on(source, hold, target):
+        for p in range(0, total, step):
+            _, spread_sum = around(source, p)
+            target[pl.ds(p + 1, step)] = hold[pl.ds(p, step)] + inv[pl.ds(p, step)] * spread_sum
+
+    def finish(source, hold, pair, keeps, only=()):
+        if pair is not None:
+            new, old, moved = pair
+            for p in range(0, total, step):
+                moved[pl.ds(p + 1, step)] = new[pl.ds(p + 1, step)] - old[pl.ds(p + 1, step)]
+        for p in range(0, total, step):
+            _, spread_sum = around(source, p)
+            value = hold[pl.ds(p, step)] + inv[pl.ds(p, step)] * spread_sum
+            if pair is not None:
+                core, spread_sum = around(moved, p)
+                value = value + (core + scale[pl.ds(p, step)] * (spread_sum - 6.0 * core))
+            for ref in keeps:
+                ref[pl.ds(p + 1, step)] = value
+            for ref in only:
+                ref[pl.ds(p + 1, step), mine] = value[:, own:2 * own]
+
+    def solve(number, start, n, ahead, pair, keeps, only=()):
+        a, b, hold = sweep.at[2 * number], sweep.at[2 * number + 1], base.at[number]
+        begin(start, n, a, hold, ahead)
+        for _ in range(SWEEPS - 2):
+            go_on(a, hold, b)
+            a, b = b, a
+        finish(a, hold, pair, keeps, only)
+
+    def deliver(n, target_s, source_t, source_s, ref):
+        return pltpu.make_async_remote_copy(
+            src_ref=ref.at[pl.ds(1 + planes * target_s, planes), mine],
+            dst_ref=out_hbm.at[0, :, block(index(source_t, source_s))],
+            send_sem=out_send.at[n, target_s],
+            recv_sem=out_recv.at[source_t, source_s],
+            device_id={"tm": n, "space": target_s},
+        )
+
+    def keep_local(n):
+        return pltpu.make_async_copy(
+            result[n].at[pl.ds(1 + planes * s, planes), mine], out_hbm.at[0, :, block(here)], last_sem.at[0]
+        )
+
+    result = [state.at[0]] + [end.at[n - 1] for n in range(1, slices)]
+
+    def emit(n):
+        for hop in range(1, count):
+            deliver(n, lax.rem(s + hop, count), t, s, result[n]).start()
+
+        @pl.when(t != n)
+        def _():
+            deliver(n, s, t, s, result[n]).start()
+
+        @pl.when(t == n)
+        def _():
+            keep_local(n).start()
+
+    starts = [given.at[0]] + [coarse.at[n - 1] for n in range(1, slices - 1)]
+    for n in range(slices - 1):
+        ahead = coarse.at[n] if n + 1 < slices - 1 else None
+        pair = (near.at[n - 1], starts[n], change.at[n - 1]) if n else None
+        keeps = (near.at[n],) if n + 1 < slices - 1 else ()
+        solve(n, starts[n], n, ahead, pair, keeps, (state.at[n],))
+        side_start(*state_side(n + 1))
+        if n == 0:
+            emit(0)
+    for n in range(1, slices):
+        side_recv_wait(*state_side(n))
+        pair = (end.at[n - 2], state.at[n - 1], change.at[slices + n - 4]) if n > 1 else None
+        keeps = (end.at[n - 1],) if n + 1 < slices else ()
+        only = () if n + 1 < slices else (end.at[n - 1],)
+        solve(slices - 2 + n, state.at[n - 1], n, None, pair, keeps, only)
+        emit(n)
+
+    for a in range(3):
+        for hop in range(1, count):
+            spread(a, lax.rem(s + hop, count), s).wait_send()
+        side_send_wait(*given_side(a))
+    for copy in ctrl_copies:
+        copy.wait_send()
+    for target in (0, 1):
+
+        @pl.when(jnp.logical_and(t == 0, s != target))
+        def _():
+            spread_seg(target, s).wait_send()
+
+    for n in range(1, slices):
+        side_send_wait(*state_side(n))
+    for n in range(slices):
+        for hop in range(1, count):
+            deliver(n, lax.rem(s + hop, count), t, s, result[n]).wait_send()
+
+        @pl.when(t != n)
+        def _():
+            deliver(n, s, t, s, result[n]).wait_send()
+
+        @pl.when(t == n)
+        def _():
+            keep_local(n).wait()
+
+    for hop_t in range(slices):
+        for hop_s in range(count):
+            if hop_t or hop_s:
+                source_t, source_s = lax.rem(t + hop_t, slices), lax.rem(s + hop_s, count)
+                deliver(t, s, source_t, source_s, result[0]).wait_recv()
+
+
+def wide_fits(slices, count, rows):
+    own = rows // (slices * count)
+    ordered = slices % 4 in (0, 2) and slices < 8 and count % 2 == 0
+    return ordered and CORRECTIONS == 2 and slices > 2 and own % 8 == 0 and own >= SWEEPS + slices - 2 \
+        and rows == own * slices * count
+
+
 def solution(mesh):
     slices, count = mesh.shape["tm"], mesh.shape["space"]
     plan = make_plan(slices)
 
+    def wide(initial_state, capacity, source, control, segment_index):
+        planes, rows, cols = initial_state.shape
+        own = rows // (slices * count)
+        total, window = planes * count, 3 * own
+        size = (planes, rows, cols, slices, count, own)
+        dma = pltpu.SemaphoreType.DMA
+
+        def fields(number):
+            return pltpu.VMEM((number, total + 2, window, cols), jnp.float32)
+
+        return pl.pallas_call(
+            functools.partial(wide_kernel, size),
+            out_shape=jax.ShapeDtypeStruct((1, planes, rows, cols), jnp.float32),
+            in_specs=[pl.BlockSpec(memory_space=pl.ANY)] * 3 + [pl.BlockSpec(memory_space=pltpu.VMEM)] * 2,
+            out_specs=pl.BlockSpec(memory_space=pl.ANY),
+            scratch_shapes=[
+                pltpu.VMEM((3, planes, rows, cols), jnp.float32),
+                fields(3),
+                pltpu.VMEM((total, window, cols), jnp.float32),
+                pltpu.VMEM((total, window, cols), jnp.float32),
+                pltpu.VMEM((slices, total, cols), jnp.float32),
+                fields(slices - 2),
+                fields(4 * (slices - 1)),
+                pltpu.VMEM((2 * (slices - 1), total, window, cols), jnp.float32),
+                fields(slices - 2),
+                fields(2 * (slices - 2)),
+                fields(slices - 1),
+                fields(slices - 1),
+                pltpu.VMEM((count,) + segment_index.shape, jnp.int32),
+                pltpu.VMEM((slices,) + control.shape, jnp.float32),
+                dma((3,)),
+                dma((5,)),
+                dma((3, count)),
+                dma((3, count)),
+                dma((count,)),
+                dma((count,)),
+                dma((slices,)),
+                dma((slices,)),
+                dma((3, 2)),
+                dma((3, 2)),
+                dma((slices - 1, 2)),
+                dma((slices - 1, 2)),
+                dma((slices, count)),
+                dma((slices, count)),
+                dma((1,)),
+            ],
+            compiler_params=pltpu.CompilerParams(
+                collective_id=0, has_side_effects=True, vmem_limit_bytes=67043328 - 1048576
+            ),
+        )(initial_state, capacity, source, control, segment_index)
+
     def on_device(initial_state, capacity, source, control, segment_index):
         planes, rows, cols = initial_state.shape
+        if wide_fits(slices, count, rows):
+            return wide(initial_state, capacity, source, control, segment_index)
         own_rows = rows // slices
         reach = -(-(CORRECTIONS * SWEEPS + slices - CORRECTIONS) // 8) * 8
         window = min(rows, own_rows + 2 * reach)

time: 63.5 us -> 44.4 us (0.70)
  the two profiles are of different devices: /device:TPU:23 before, /device:TPU:7 now
where the time goes in v1:
time: 44.4 us; the launch traced here: 44.2 us
  Pallas kernels  42.3 us (95%)
  local copies, waits for them, and re-layouts  1.87 us (4%)
    pallas_call x1, Pallas kernels, wide(): pl.pallas_call(functools.partial(wide_kernel, size), out_shape=jax.ShapeD...  42.3 us
    unnamed x1, local copies, waits for them, and re-layouts  1.87 us

profile of v1, /device:TPU:7, one launch (start us, length us, event | category | flops | bytes accessed | tf_op | source)
XLA Modules:
  0.0 44.2 jit_solution(13159838574620502646)
XLA Ops:
  0.0 42.3 %shard_map.55 = f32[1,2,256,256]{3,2,1,0:T(8,128)} custom-call(f32[2,256,256]{2,1,0:T(8,128)} %state_hbm.1, f32[2,256,256]{2,1,0:T(8,128)} %cap_hbm.1, f32[2,256,256]{2,1,0:T(8,128)} %src_hbm.1, f32[1,16]{1,0:T(1,128)} %ctrl_ref.1, s32[2,256]{1,0:T(2,128)} %seg_ref.1), custom_call_target="tpu_custom_call" | custom-call | tf_op jit(solution)/shard_map/pallas_call | solution.py:662
  42.4 1.9 %copy.7 = f32[1,2,256,256]{3,2,1,0:T(8,128)} copy(f32[1,2,256,256]{3,2,1,0:T(8,128)} %shard_map.55) | data formatting | bytes 1048576

commit v2 on v1

--- a/solution.py
+++ b/solution.py
@@ -305,8 +305,9 @@
     planes, rows, cols, slices, count, own = size
     total = planes * count
     devices = slices * count
-    window = 3 * own
-    mine = pl.ds(own, own)
+    window, pad, lanes = 3 * own, 8, 128
+    parts = cols // lanes
+    mine = pl.ds(pad + own, own)
     whole = pl.ds(1, total)
     t = lax.axis_index("tm")
     s = lax.axis_index("space")
@@ -334,19 +335,32 @@
 
     inputs = (state_hbm, cap_hbm, src_hbm)
     order = (1, 0, 2)
-    loads = [pltpu.make_async_copy(inputs[a], stage.at[a], load_sem.at[a]) for a in range(3)]
-    owns = [
-        pltpu.make_async_copy(
-            inputs[a].at[:, block(here)], given.at[a, pl.ds(1 + planes * s, planes), mine], own_sem.at[a]
-        )
+    loads = [
+        [
+            pltpu.make_async_copy(
+                inputs[a].at[:, :, pl.ds(h * lanes, lanes)], stage.at[a, :, h], load_sem.at[a, h]
+            )
+            for h in range(parts)
+        ]
         for a in range(3)
     ]
-    for a in order:
-        loads[a].start()
-    for a in order:
-        owns[a].start()
-    own_seg = pltpu.make_async_copy(seg_ref, seg_all.at[s], own_sem.at[3])
-    own_ctrl = pltpu.make_async_copy(ctrl_ref, ctrl_all.at[0], own_sem.at[4])
+    owns = [
+        [
+            pltpu.make_async_copy(
+                inputs[a].at[:, block(here), pl.ds(h * lanes, lanes)],
+                given.at[a, pl.ds(1 + planes * s, planes), h, mine],
+                own_sem.at[a, h],
+            )
+            for h in range(parts)
+        ]
+        for a in range(3)
+    ]
+    for group in (loads, owns):
+        for a in order:
+            for copy in group[a]:
+                copy.start()
+    own_seg = pltpu.make_async_copy(seg_ref, seg_all.at[s], last_sem.at[1])
+    own_ctrl = pltpu.make_async_copy(ctrl_ref, ctrl_all.at[0], last_sem.at[2])
 
     seg_all[...] = jnp.zeros(seg_all.shape, jnp.int32)
     barrier = pltpu.get_barrier_semaphore()
@@ -355,29 +369,29 @@
     for hop in range(1, slices):
         pl.semaphore_signal(barrier, inc=1, device_id={"tm": lax.rem(t + hop, slices)})
 
-    flat = jnp.zeros((window, cols), jnp.float32)
+    flat = jnp.zeros((parts, window + 2 * pad, lanes), jnp.float32)
     for plane in (0, total + 1):
         given[0, plane] = flat
-        for ref in (coarse, sweep, near, change, state, end):
+        for ref in (coarse, sweep, change, state):
             for k in range(ref.shape[0]):
                 ref[k, plane] = flat
-    for missing, at in ((has_low, 0), (has_high, 2 * own)):
+    for missing, at in ((has_low, pad), (has_high, pad + 2 * own)):
 
         @pl.when(jnp.logical_not(missing))
         def _():
-            side = jnp.zeros((total, own, cols), jnp.float32)
-            given[0, whole, pl.ds(at, own)] = side
-            given[1, whole, pl.ds(at, own)] = side + 1.0
-            given[2, whole, pl.ds(at, own)] = side
+            side = jnp.zeros((total, parts, own, lanes), jnp.float32)
+            given[0, whole, :, pl.ds(at, own)] = side
+            given[1, whole, :, pl.ds(at, own)] = side + 1.0
+            given[2, whole, :, pl.ds(at, own)] = side
             for k in range(state.shape[0]):
-                state[k, whole, pl.ds(at, own)] = side
+                state[k, whole, :, pl.ds(at, own)] = side
 
     pl.semaphore_wait(barrier, slices + count - 2)
 
     def spread(a, target, source):
         return pltpu.make_async_remote_copy(
-            src_ref=stage.at[a, :, block(index(t, target))],
-            dst_ref=given.at[a, pl.ds(1 + planes * source, planes), mine],
+            src_ref=stage.at[a, :, :, block(index(t, target))],
+            dst_ref=given.at[a, pl.ds(1 + planes * source, planes), :, mine],
             send_sem=in_send.at[a, target],
             recv_sem=in_recv.at[a, source],
             device_id={"space": target},
@@ -392,11 +406,11 @@
             device_id={"space": target},
         )
 
-    def side(make, send_sem, recv_sem, upward):
+    def side(origin, target, send_sem, recv_sem, upward):
         other_t, other_s = place(here + 1 if upward else here - 1)
         return pltpu.make_async_remote_copy(
-            src_ref=make(own),
-            dst_ref=make(0 if upward else 2 * own),
+            src_ref=origin.at[whole, :, mine],
+            dst_ref=target.at[whole, :, pl.ds(pad if upward else pad + 2 * own, own)],
             send_sem=send_sem.at[int(upward)],
             recv_sem=recv_sem.at[int(upward)],
             device_id={"tm": other_t, "space": other_s},
@@ -424,13 +438,14 @@
                 side(*args, upward).wait_send()
 
     def given_side(a):
-        return lambda at: given.at[a, whole, pl.ds(at, own)], side_send.at[a], side_recv.at[a]
+        return given.at[a], given.at[a], side_send.at[a], side_recv.at[a]
 
     def state_side(n):
-        return lambda at: state.at[n - 1, whole, pl.ds(at, own)], mid_send.at[n - 1], mid_recv.at[n - 1]
+        return near.at[n - 1], state.at[n - 1], mid_send.at[n - 1], mid_recv.at[n - 1]
 
     for a in order:
-        loads[a].wait()
+        for copy in loads[a]:
+            copy.wait()
         for hop in range(1, count):
             target = lax.rem(s + hop, count)
             spread(a, target, s).start()
@@ -453,13 +468,14 @@
                 def _():
                     spread_seg(target, s).start()
 
-    row_id = lax.broadcasted_iota(jnp.int32, (window, cols), 0) + (here - 1) * own
+    step = 2
+    row_id = lax.broadcasted_iota(jnp.int32, (step, parts, window, lanes), 2) + (here - 1) * own
     inside = jnp.logical_and(row_id >= 0, row_id < rows)
-    step = planes
-    spans = [pl.ds(p, step) for p in range(0, total, step)]
+    all_rows = pl.ds(pad, window)
 
     def collect(a):
-        owns[a].wait()
+        for copy in owns[a]:
+            copy.wait()
         for hop in range(1, count):
             source = lax.rem(s + count - hop, count)
             spread(a, s, source).wait_recv()
@@ -469,9 +485,9 @@
     collect(0)
     side_recv_wait(*given_side(1))
     for p in range(0, total, step):
-        capacity = given[1, pl.ds(p + 1, step)]
-        scale[pl.ds(p, step)] = jnp.where(inside, step_coarse / capacity, 0.0)
-        inv[pl.ds(p, step)] = jnp.where(inside, 1.0 / (capacity + 6.0 * step_fine), 0.0)
+        capacity = given[1, pl.ds(p + 1, step), :, all_rows]
+        scale[pl.ds(p, step), :, all_rows] = jnp.where(inside, step_coarse / capacity, 0.0)
+        inv[pl.ds(p, step), :, all_rows] = jnp.where(inside, 1.0 / (capacity + 6.0 * step_fine), 0.0)
 
     own_seg.wait()
     own_ctrl.wait()
@@ -495,75 +511,110 @@
             values = jnp.zeros((planes, cols), jnp.float32)
             for k in range(segments):
                 values = jnp.where(segment == k, row[:, k:k + 1], values)
-            bounds[n, pl.ds(source * planes, planes)] = values
+            for plane in range(planes):
+                for h in range(parts):
+                    bounds[n, source * planes + plane, h] = jnp.broadcast_to(
+                        values[plane:plane + 1, h * lanes:(h + 1) * lanes], (8, lanes)
+                    )
 
     collect(2)
     side_recv_wait(*given_side(0))
     side_recv_wait(*given_side(2))
 
-    half = cols // 2
-    lane = lax.broadcasted_iota(jnp.int32, (step, window, half), 2)
-    first_row = row_id == 0
-
-    def around(ref, p):
-        core = ref[pl.ds(p + 1, step)]
-        result = ref[pl.ds(p, step)] + ref[pl.ds(p + 2, step)]
-        result = result + (pltpu.roll(core, 1, 1) + pltpu.roll(core, window - 1, 1))
-        left, right = core[:, :, :half], core[:, :, half:]
-        left_up, right_up = pltpu.roll(left, 1, 2), pltpu.roll(right, 1, 2)
-        left_down, right_down = pltpu.roll(left, half - 1, 2), pltpu.roll(right, half - 1, 2)
-        low = jnp.where(lane == 0, 0.0, left_up) + jnp.where(lane == half - 1, right_down, left_down)
-        high = jnp.where(lane == 0, left_up, right_up) + jnp.where(lane == half - 1, 0.0, right_down)
-        return core, result + jnp.concatenate([low, high], axis=2)
-
-    def forcing(n, p):
-        edge = bounds[n, pl.ds(p, step)][:, None, :]
-        return given[2, pl.ds(p + 1, step)] + jnp.where(first_row[None], edge, 0.0)
-
-    def begin(start, n, target, hold, ahead=None):
+    lane = lax.broadcasted_iota(jnp.int32, (step, 8, lanes), 2)
+    lane_low, lane_high = lane == 0, lane == lanes - 1
+
+    def extent(reach):
+        extra = -(-reach // 4) * 4
+        return own - extra, own + 2 * extra
+
+    def load(ref, p, h, at, height):
+        return ref[pl.ds(p, step), h, pl.ds(pad + at, height)]
+
+    def rotate(value, amount):
+        return pltpu.roll(value, amount % lanes, 2)
+
+    def around(ref, p, at, height):
+        cores, sums = [], []
+        for h in range(parts):
+            block = ref[pl.ds(p, step + 2), h, pl.ds(pad + at, height)]
+            cores.append(block[1:step + 1])
+            sums.append(block[:step] + block[2:] + (
+                load(ref, p + 1, h, at - 1, height) + load(ref, p + 1, h, at + 1, height)
+            ))
+        ups = [rotate(core, 1) for core in cores]
+        downs = [rotate(core, -1) for core in cores]
+        low = jnp.concatenate([lane_low] * (height // 8), axis=1)
+        high = jnp.concatenate([lane_high] * (height // 8), axis=1)
+        for h in range(parts):
+            left = jnp.where(low, ups[h - 1] if h else 0.0, ups[h])
+            right = jnp.where(high, downs[h + 1] if h + 1 < parts else 0.0, downs[h])
+            sums[h] = sums[h] + (left + right)
+        return cores, sums
+
+    def row_mask(at, height):
+        row_id = lax.broadcasted_iota(jnp.int32, (step, height, lanes), 1) + ((here - 1) * own + at)
+        return row_id == 0
+
+    def begin(start, n, target, hold, ahead, reach):
+        at, height = extent(reach)
+        first_row = row_mask(at, height)
         for p in range(0, total, step):
-            core, spread_sum = around(start, p)
-            gain = inv[pl.ds(p, step)]
-            drive = forcing(n, p) - 6.0 * step_fine * core
-            constant = core + gain * drive
-            hold[pl.ds(p, step)] = constant
-            target[pl.ds(p + 1, step)] = constant + gain * spread_sum
-            if ahead is not None:
-                ahead[pl.ds(p + 1, step)] = core + scale[pl.ds(p, step)] * (drive + spread_sum)
-
-    def go_on(source, hold, target):
+            cores, sums = around(start, p, at, height)
+            for h in range(parts):
+                edge = jnp.concatenate([bounds[n, pl.ds(p, step), h]] * (height // 8), axis=1)
+                gain = load(inv, p, h, at, height)
+                drive = load(given.at[2], p + 1, h, at, height) + jnp.where(first_row, edge, 0.0)
+                drive = drive - 6.0 * step_fine * cores[h]
+                constant = cores[h] + gain * drive
+                hold[pl.ds(p, step), h, pl.ds(pad + at, height)] = constant
+                target[pl.ds(p + 1, step), h, pl.ds(pad + at, height)] = constant + gain * sums[h]
+                if ahead is not None:
+                    ahead[pl.ds(p + 1, step), h, pl.ds(pad + at, height)] = cores[h] + load(
+                        scale, p, h, at, height
+                    ) * (drive + sums[h])
+
+    def go_on(source, hold, target, reach):
+        at, height = extent(reach)
         for p in range(0, total, step):
-            _, spread_sum = around(source, p)
-            target[pl.ds(p + 1, step)] = hold[pl.ds(p, step)] + inv[pl.ds(p, step)] * spread_sum
-
-    def finish(source, hold, pair, keeps, only=()):
+            _, sums = around(source, p, at, height)
+            for h in range(parts):
+                target[pl.ds(p + 1, step), h, pl.ds(pad + at, height)] = load(
+                    hold, p, h, at, height
+                ) + load(inv, p, h, at, height) * sums[h]
+
+    def finish(source, hold, pair, target, reach):
         if pair is not None:
             new, old, moved = pair
+            at, height = extent(reach + 1)
             for p in range(0, total, step):
-                moved[pl.ds(p + 1, step)] = new[pl.ds(p + 1, step)] - old[pl.ds(p + 1, step)]
+                for h in range(parts):
+                    moved[pl.ds(p + 1, step), h, pl.ds(pad + at, height)] = load(
+                        new, p + 1, h, at, height
+                    ) - load(old, p + 1, h, at, height)
+        at, height = extent(reach)
         for p in range(0, total, step):
-            _, spread_sum = around(source, p)
-            value = hold[pl.ds(p, step)] + inv[pl.ds(p, step)] * spread_sum
+            _, sums = around(source, p, at, height)
             if pair is not None:
-                core, spread_sum = around(moved, p)
-                value = value + (core + scale[pl.ds(p, step)] * (spread_sum - 6.0 * core))
-            for ref in keeps:
-                ref[pl.ds(p + 1, step)] = value
-            for ref in only:
-                ref[pl.ds(p + 1, step), mine] = value[:, own:2 * own]
-
-    def solve(number, start, n, ahead, pair, keeps, only=()):
+                cores, spreads = around(moved, p, at, height)
+            for h in range(parts):
+                value = load(hold, p, h, at, height) + load(inv, p, h, at, height) * sums[h]
+                if pair is not None:
+                    value = value + (cores[h] + load(scale, p, h, at, height) * (spreads[h] - 6.0 * cores[h]))
+                target[pl.ds(p + 1, step), h, pl.ds(pad + at, height)] = value
+
+    def solve(number, start, n, ahead, pair, target, reach):
         a, b, hold = sweep.at[2 * number], sweep.at[2 * number + 1], base.at[number]
-        begin(start, n, a, hold, ahead)
-        for _ in range(SWEEPS - 2):
-            go_on(a, hold, b)
+        begin(start, n, a, hold, ahead, reach + SWEEPS - 1)
+        for j in range(2, SWEEPS):
+            go_on(a, hold, b, reach + SWEEPS - j)
             a, b = b, a
-        finish(a, hold, pair, keeps, only)
+        finish(a, hold, pair, target, reach)
 
     def deliver(n, target_s, source_t, source_s, ref):
         return pltpu.make_async_remote_copy(
-            src_ref=ref.at[pl.ds(1 + planes * target_s, planes), mine],
-            dst_ref=out_hbm.at[0, :, block(index(source_t, source_s))],
+            src_ref=ref.at[pl.ds(1 + planes * target_s, planes), :, mine],
+            dst_ref=out_hbm.at[:, index(source_t, source_s)],
             send_sem=out_send.at[n, target_s],
             recv_sem=out_recv.at[source_t, source_s],
             device_id={"tm": n, "space": target_s},
@@ -571,10 +622,10 @@
 
     def keep_local(n):
         return pltpu.make_async_copy(
-            result[n].at[pl.ds(1 + planes * s, planes), mine], out_hbm.at[0, :, block(here)], last_sem.at[0]
+            result[n].at[pl.ds(1 + planes * s, planes), :, mine], out_hbm.at[:, here], last_sem.at[0]
         )
 
-    result = [state.at[0]] + [end.at[n - 1] for n in range(1, slices)]
+    result = [near.at[0]] + [end.at[n - 1] for n in range(1, slices)]
 
     def emit(n):
         for hop in range(1, count):
@@ -590,19 +641,18 @@
 
     starts = [given.at[0]] + [coarse.at[n - 1] for n in range(1, slices - 1)]
     for n in range(slices - 1):
-        ahead = coarse.at[n] if n + 1 < slices - 1 else None
+        ahead = coarse.at[n] if n + 2 < slices else None
         pair = (near.at[n - 1], starts[n], change.at[n - 1]) if n else None
-        keeps = (near.at[n],) if n + 1 < slices - 1 else ()
-        solve(n, starts[n], n, ahead, pair, keeps, (state.at[n],))
+        solve(n, starts[n], n, ahead, pair, near.at[n], slices - 2 - n)
         side_start(*state_side(n + 1))
         if n == 0:
             emit(0)
+        for p in range(0, total, step):
+            state[n, pl.ds(p + 1, step), :, mine] = near[n, pl.ds(p + 1, step), :, mine]
     for n in range(1, slices):
         side_recv_wait(*state_side(n))
         pair = (end.at[n - 2], state.at[n - 1], change.at[slices + n - 4]) if n > 1 else None
-        keeps = (end.at[n - 1],) if n + 1 < slices else ()
-        only = () if n + 1 < slices else (end.at[n - 1],)
-        solve(slices - 2 + n, state.at[n - 1], n, None, pair, keeps, only)
+        solve(slices - 2 + n, state.at[n - 1], n, None, pair, end.at[n - 1], slices - 1 - n)
         emit(n)
 
     for a in range(3):
@@ -638,11 +688,11 @@
                 deliver(t, s, source_t, source_s, result[0]).wait_recv()
 
 
-def wide_fits(slices, count, rows):
+def wide_fits(slices, count, rows, cols):
     own = rows // (slices * count)
     ordered = slices % 4 in (0, 2) and slices < 8 and count % 2 == 0
-    return ordered and CORRECTIONS == 2 and slices > 2 and own % 8 == 0 and own >= SWEEPS + slices - 2 \
-        and rows == own * slices * count
+    return ordered and CORRECTIONS == 2 and slices > 2 and own == 8 and own >= SWEEPS + slices - 2 \
+        and rows == own * slices * count and cols % 128 == 0
 
 
 def solution(mesh):
@@ -652,35 +702,36 @@
     def wide(initial_state, capacity, source, control, segment_index):
         planes, rows, cols = initial_state.shape
         own = rows // (slices * count)
-        total, window = planes * count, 3 * own
+        total, window, parts = planes * count, 3 * own, cols // 128
+        still = (total, parts, window + 16, 128)
         size = (planes, rows, cols, slices, count, own)
         dma = pltpu.SemaphoreType.DMA
 
         def fields(number):
-            return pltpu.VMEM((number, total + 2, window, cols), jnp.float32)
-
-        return pl.pallas_call(
+            return pltpu.VMEM((number, total + 2, parts, window + 16, 128), jnp.float32)
+
+        result = pl.pallas_call(
             functools.partial(wide_kernel, size),
-            out_shape=jax.ShapeDtypeStruct((1, planes, rows, cols), jnp.float32),
+            out_shape=jax.ShapeDtypeStruct((planes, rows // own, parts, own, 128), jnp.float32),
             in_specs=[pl.BlockSpec(memory_space=pl.ANY)] * 3 + [pl.BlockSpec(memory_space=pltpu.VMEM)] * 2,
             out_specs=pl.BlockSpec(memory_space=pl.ANY),
             scratch_shapes=[
-                pltpu.VMEM((3, planes, rows, cols), jnp.float32),
+                pltpu.VMEM((3, planes, parts, rows, 128), jnp.float32),
                 fields(3),
-                pltpu.VMEM((total, window, cols), jnp.float32),
-                pltpu.VMEM((total, window, cols), jnp.float32),
-                pltpu.VMEM((slices, total, cols), jnp.float32),
+                pltpu.VMEM(still, jnp.float32),
+                pltpu.VMEM(still, jnp.float32),
+                pltpu.VMEM((slices, total, parts, 8, 128), jnp.float32),
                 fields(slices - 2),
                 fields(4 * (slices - 1)),
-                pltpu.VMEM((2 * (slices - 1), total, window, cols), jnp.float32),
-                fields(slices - 2),
+                pltpu.VMEM((2 * (slices - 1),) + still, jnp.float32),
+                fields(slices - 1),
                 fields(2 * (slices - 2)),
                 fields(slices - 1),
                 fields(slices - 1),
                 pltpu.VMEM((count,) + segment_index.shape, jnp.int32),
                 pltpu.VMEM((slices,) + control.shape, jnp.float32),
-                dma((3,)),
-                dma((5,)),
+                dma((3, parts)),
+                dma((3, parts)),
                 dma((3, count)),
                 dma((3, count)),
                 dma((count,)),
@@ -693,16 +744,17 @@
                 dma((slices - 1, 2)),
                 dma((slices, count)),
                 dma((slices, count)),
-                dma((1,)),
+                dma((3,)),
             ],
             compiler_params=pltpu.CompilerParams(
                 collective_id=0, has_side_effects=True, vmem_limit_bytes=67043328 - 1048576
             ),
         )(initial_state, capacity, source, control, segment_index)
+        return result.transpose(0, 1, 3, 2, 4).reshape(1, planes, rows, cols)
 
     def on_device(initial_state, capacity, source, control, segment_index):
         planes, rows, cols = initial_state.shape
-        if wide_fits(slices, count, rows):
+        if wide_fits(slices, count, rows, cols):
             return wide(initial_state, capacity, source, control, segment_index)
         own_rows = rows // slices
         reach = -(-(CORRECTIONS * SWEEPS + slices - CORRECTIONS) // 8) * 8

time: 44.4 us -> 43.9 us (0.989)
  Pallas kernels: 42.3 us -> 41.8 us
    pallas_call x1, Pallas kernels: 42.3 us -> 41.8 us  [wide(): pl.pallas_call(functools.partial(wide_kernel, size), out_shape=jax.ShapeD...]
where the time goes in v2:
time: 43.9 us; the launch traced here: 43.7 us
  Pallas kernels  41.8 us (95%)
  local copies, waits for them, and re-layouts  1.87 us (4%)
    pallas_call x1, Pallas kernels, wide(): pl.pallas_call(functools.partial(wide_kernel, size), out_shape=jax.ShapeD...  41.8 us
    unnamed x1, local copies, waits for them, and re-layouts  1.87 us

profile of v2, /device:TPU:7, one launch (start us, length us, event | category | flops | bytes accessed | tf_op | source)
XLA Modules:
  0.0 43.7 jit_solution(11316568214274173036)
XLA Ops:
  0.0 41.8 %shard_map.55 = f32[2,32,2,8,128]{4,3,2,1,0:T(8,128)} custom-call(f32[2,256,256]{2,1,0:T(8,128)} %state_hbm.1, f32[2,256,256]{2,1,0:T(8,128)} %cap_hbm.1, f32[2,256,256]{2,1,0:T(8,128)} %src_hbm.1, f32[1,16]{1,0:T(1,128)} %ctrl_ref.1, s32[2,256]{1,0:T(2,128)} %seg_ref.1), custom_call_target="tpu_custom_call" | custom-call | tf_op jit(solution)/shard_map/pallas_call | solution.py:713
  41.8 1.9 %copy.7 = f32[1,2,256,256]{3,2,1,0:T(8,128)} copy(f32[1,2,256,256]{3,2,1,0:T(8,128)} %bitcast.3) | data formatting | bytes 1048576

commit v3 on v2

--- a/solution.py
+++ b/solution.py
@@ -301,7 +301,7 @@
                 stage, given, inv, scale, bounds, coarse, sweep, base, near, change, state, end,
                 seg_all, ctrl_all, load_sem, own_sem, in_send, in_recv, seg_send, seg_recv,
                 ctrl_send, ctrl_recv, side_send, side_recv, mid_send, mid_recv,
-                out_send, out_recv, last_sem):
+                out_send, out_recv, last_sem, level_sem, ring_sem):
     planes, rows, cols, slices, count, own = size
     total = planes * count
     devices = slices * count
@@ -363,11 +363,26 @@
     own_ctrl = pltpu.make_async_copy(ctrl_ref, ctrl_all.at[0], last_sem.at[2])
 
     seg_all[...] = jnp.zeros(seg_all.shape, jnp.int32)
+    levels = count // 2
+    level, core = s // 2, s % 2
+    spot = swap(t)
+    ring_ids = [{"tm": swap(lax.rem(spot + hop, slices))} for hop in (1, slices - 1)]
+    has_down, has_up = level > 0, level < levels - 1
+    beside = jnp.minimum(level, 1) + jnp.minimum(levels - 1 - level, 1)
+
+    def signal_levels(semaphore):
+        for there, shift in ((has_down, -1), (has_up, 1)):
+
+            @pl.when(there)
+            def _():
+                for other in (0, 1):
+                    pl.semaphore_signal(semaphore, inc=1, device_id={"space": 2 * (level + shift) + other})
+
     barrier = pltpu.get_barrier_semaphore()
-    for hop in range(1, count):
-        pl.semaphore_signal(barrier, inc=1, device_id={"space": lax.rem(s + hop, count)})
-    for hop in range(1, slices):
-        pl.semaphore_signal(barrier, inc=1, device_id={"tm": lax.rem(t + hop, slices)})
+    signal_levels(barrier)
+    pl.semaphore_signal(barrier, inc=1, device_id={"space": s + 1 - 2 * core})
+    for ring_id in ring_ids:
+        pl.semaphore_signal(barrier, inc=1, device_id=ring_id)
 
     flat = jnp.zeros((parts, window + 2 * pad, lanes), jnp.float32)
     for plane in (0, total + 1):
@@ -386,7 +401,7 @@
             for k in range(state.shape[0]):
                 state[k, whole, :, pl.ds(at, own)] = side
 
-    pl.semaphore_wait(barrier, slices + count - 2)
+    pl.semaphore_wait(barrier, 3 + 2 * beside)
 
     def spread(a, target, source):
         return pltpu.make_async_remote_copy(
@@ -443,30 +458,47 @@
     def state_side(n):
         return near.at[n - 1], state.at[n - 1], mid_send.at[n - 1], mid_recv.at[n - 1]
 
-    for a in order:
+    def spread_far(a, distance):
+        for shift in (-distance, distance):
+            there = jnp.logical_and(level + shift >= 0, level + shift < levels)
+
+            @pl.when(there)
+            def _():
+                for other in (0, 1):
+                    spread(a, 2 * (level + shift) + other, s).start()
+
+    def spread_near(a):
         for copy in loads[a]:
             copy.wait()
-        for hop in range(1, count):
-            target = lax.rem(s + hop, count)
-            spread(a, target, s).start()
-        if a == order[0]:
-            own_seg.start()
-            own_ctrl.start()
-            ctrl_copies = []
-            for hop in range(1, slices):
-                ctrl_copies.append(pltpu.make_async_remote_copy(
-                    src_ref=ctrl_ref,
-                    dst_ref=ctrl_all.at[hop],
-                    send_sem=ctrl_send.at[hop],
-                    recv_sem=ctrl_recv.at[hop],
-                    device_id={"tm": lax.rem(t + hop, slices)},
-                ))
-                ctrl_copies[-1].start()
-            for target in (0, 1):
-
-                @pl.when(jnp.logical_and(t == 0, s != target))
-                def _():
-                    spread_seg(target, s).start()
+        spread_far(a, 1)
+        spread(a, s + 1 - 2 * core, s).start()
+
+    def pass_ctrl(step):
+        return pltpu.make_async_remote_copy(
+            src_ref=ctrl_all.at[step - 1] if step > 1 else ctrl_ref,
+            dst_ref=ctrl_all.at[step],
+            send_sem=ctrl_send.at[step],
+            recv_sem=ctrl_recv.at[step],
+            device_id=ring_ids[0],
+        )
+
+    spread_near(order[0])
+    if levels > 2:
+        signal_levels(level_sem.at[0])
+    spread_near(order[1])
+    for distance in range(2, levels):
+        pl.semaphore_wait(level_sem.at[distance - 2], 2 * beside)
+        if distance + 1 < levels:
+            signal_levels(level_sem.at[distance - 1])
+        spread_far(order[0], distance)
+    for distance in range(2, levels):
+        spread_far(order[1], distance)
+    spread_near(order[2])
+    for distance in range(2, levels):
+        spread_far(order[2], distance)
+    own_seg.start()
+    own_ctrl.start()
+    pass_ctrl(1).start()
 
     step = 2
     row_id = lax.broadcasted_iota(jnp.int32, (step, parts, window, lanes), 2) + (here - 1) * own
@@ -482,6 +514,17 @@
         side_start(*given_side(a))
 
     collect(1)
+    for ring_id in ring_ids:
+        pl.semaphore_signal(ring_sem.at[0], inc=1, device_id=ring_id)
+    for target in (0, 1):
+
+        @pl.when(jnp.logical_and(t == 0, s != target))
+        def _():
+            spread_seg(target, s).start()
+
+    for hop in range(1, slices - 1):
+        pass_ctrl(hop).wait_recv()
+        pass_ctrl(hop + 1).start()
     collect(0)
     side_recv_wait(*given_side(1))
     for p in range(0, total, step):
@@ -491,8 +534,7 @@
 
     own_seg.wait()
     own_ctrl.wait()
-    for copy in ctrl_copies:
-        copy.wait_recv()
+    pass_ctrl(slices - 1).wait_recv()
     for target in (0, 1):
 
         @pl.when(jnp.logical_and(t == 0, s == target))
@@ -505,7 +547,7 @@
     for n in range(slices):
         row = jnp.zeros((1, segments), jnp.float32)
         for hop in range(slices):
-            row = jnp.where(lax.rem(t - n + slices, slices) == hop, ctrl_all[hop], row)
+            row = jnp.where(lax.rem(spot - swap(n) + slices, slices) == hop, ctrl_all[hop], row)
         for source in range(count):
             segment = seg_all[source]
             values = jnp.zeros((planes, cols), jnp.float32)
@@ -645,10 +687,14 @@
         pair = (near.at[n - 1], starts[n], change.at[n - 1]) if n else None
         solve(n, starts[n], n, ahead, pair, near.at[n], slices - 2 - n)
         side_start(*state_side(n + 1))
-        if n == 0:
-            emit(0)
         for p in range(0, total, step):
             state[n, pl.ds(p + 1, step), :, mine] = near[n, pl.ds(p + 1, step), :, mine]
+    for far in range(1, slices // 2):
+        pl.semaphore_wait(ring_sem.at[far - 1], 2)
+        for ring_id in ring_ids:
+            pl.semaphore_signal(ring_sem.at[far], inc=1, device_id=ring_id)
+    pl.semaphore_wait(ring_sem.at[slices // 2 - 1], 2)
+    emit(0)
     for n in range(1, slices):
         side_recv_wait(*state_side(n))
         pair = (end.at[n - 2], state.at[n - 1], change.at[slices + n - 4]) if n > 1 else None
@@ -659,8 +705,8 @@
         for hop in range(1, count):
             spread(a, lax.rem(s + hop, count), s).wait_send()
         side_send_wait(*given_side(a))
-    for copy in ctrl_copies:
-        copy.wait_send()
+    for hop in range(1, slices):
+        pass_ctrl(hop).wait_send()
     for target in (0, 1):
 
         @pl.when(jnp.logical_and(t == 0, s != target))
@@ -745,6 +791,8 @@
                 dma((slices, count)),
                 dma((slices, count)),
                 dma((3,)),
+                pltpu.SemaphoreType.REGULAR((max(count // 2 - 2, 1),)),
+                pltpu.SemaphoreType.REGULAR((slices // 2,)),
             ],
             compiler_params=pltpu.CompilerParams(
                 collective_id=0, has_side_effects=True, vmem_limit_bytes=67043328 - 1048576

time: 43.9 us -> 43.4 us (0.989)
  no operation moved by 1% of the time
where the time goes in v3:
time: 43.4 us; the launch traced here: 43.3 us
  Pallas kernels  41.4 us (95%)
  local copies, waits for them, and re-layouts  1.87 us (4%)
    pallas_call x1, Pallas kernels, wide(): pl.pallas_call(functools.partial(wide_kernel, size), out_shape=jax.ShapeD...  41.4 us
    unnamed x1, local copies, waits for them, and re-layouts  1.87 us

profile of v3, /device:TPU:7, one launch (start us, length us, event | category | flops | bytes accessed | tf_op | source)
XLA Modules:
  0.0 43.3 jit_solution(7417225407861113533)
XLA Ops:
  0.0 41.4 %shard_map.55 = f32[2,32,2,8,128]{4,3,2,1,0:T(8,128)} custom-call(f32[2,256,256]{2,1,0:T(8,128)} %state_hbm.1, f32[2,256,256]{2,1,0:T(8,128)} %cap_hbm.1, f32[2,256,256]{2,1,0:T(8,128)} %src_hbm.1, f32[1,16]{1,0:T(1,128)} %ctrl_ref.1, s32[2,256]{1,0:T(2,128)} %seg_ref.1), custom_call_target="tpu_custom_call" | custom-call | tf_op jit(solution)/shard_map/pallas_call | solution.py:759
  41.4 1.9 %copy.7 = f32[1,2,256,256]{3,2,1,0:T(8,128)} copy(f32[1,2,256,256]{3,2,1,0:T(8,128)} %bitcast.3) | data formatting | bytes 1048576

commit v4 on v3

--- a/solution.py
+++ b/solution.py
@@ -482,6 +482,8 @@
             device_id=ring_ids[0],
         )
 
+    own_ctrl.start()
+    pass_ctrl(1).start()
     spread_near(order[0])
     if levels > 2:
         signal_levels(level_sem.at[0])
@@ -497,8 +499,8 @@
     for distance in range(2, levels):
         spread_far(order[2], distance)
     own_seg.start()
-    own_ctrl.start()
-    pass_ctrl(1).start()
+    pass_ctrl(1).wait_recv()
+    pass_ctrl(2).start()
 
     step = 2
     row_id = lax.broadcasted_iota(jnp.int32, (step, parts, window, lanes), 2) + (here - 1) * own
@@ -522,10 +524,14 @@
         def _():
             spread_seg(target, s).start()
 
-    for hop in range(1, slices - 1):
+    for hop in range(2, slices - 1):
         pass_ctrl(hop).wait_recv()
         pass_ctrl(hop + 1).start()
     collect(0)
+    for far in range(1, slices // 2):
+        pl.semaphore_wait(ring_sem.at[far - 1], 2)
+        for ring_id in ring_ids:
+            pl.semaphore_signal(ring_sem.at[far], inc=1, device_id=ring_id)
     side_recv_wait(*given_side(1))
     for p in range(0, total, step):
         capacity = given[1, pl.ds(p + 1, step), :, all_rows]
@@ -689,10 +695,6 @@
         side_start(*state_side(n + 1))
         for p in range(0, total, step):
             state[n, pl.ds(p + 1, step), :, mine] = near[n, pl.ds(p + 1, step), :, mine]
-    for far in range(1, slices // 2):
-        pl.semaphore_wait(ring_sem.at[far - 1], 2)
-        for ring_id in ring_ids:
-            pl.semaphore_signal(ring_sem.at[far], inc=1, device_id=ring_id)
     pl.semaphore_wait(ring_sem.at[slices // 2 - 1], 2)
     emit(0)
     for n in range(1, slices):

time: 43.4 us -> 43.3 us (level)
  no operation moved by 1% of the time
where the time goes in v4:
time: 43.3 us; the launch traced here: 43.1 us
  Pallas kernels  41.2 us (95%)
  local copies, waits for them, and re-layouts  1.87 us (4%)
    pallas_call x1, Pallas kernels, wide(): pl.pallas_call(functools.partial(wide_kernel, size), out_shape=jax.ShapeD...  41.2 us
    unnamed x1, local copies, waits for them, and re-layouts  1.87 us

profile of v4, /device:TPU:7, one launch (start us, length us, event | category | flops | bytes accessed | tf_op | source)
XLA Modules:
  0.0 43.1 jit_solution(17417788691002859593)
XLA Ops:
  0.0 41.2 %shard_map.55 = f32[2,32,2,8,128]{4,3,2,1,0:T(8,128)} custom-call(f32[2,256,256]{2,1,0:T(8,128)} %state_hbm.1, f32[2,256,256]{2,1,0:T(8,128)} %cap_hbm.1, f32[2,256,256]{2,1,0:T(8,128)} %src_hbm.1, f32[1,16]{1,0:T(1,128)} %ctrl_ref.1, s32[2,256]{1,0:T(2,128)} %seg_ref.1), custom_call_target="tpu_custom_call" | custom-call | tf_op jit(solution)/shard_map/pallas_call | solution.py:761
  41.2 1.9 %copy.7 = f32[1,2,256,256]{3,2,1,0:T(8,128)} copy(f32[1,2,256,256]{3,2,1,0:T(8,128)} %bitcast.3) | data formatting | bytes 1048576
